TPU v7x, 128 devices: a whole 4x4x4 slice. The times are simulated.
128 devices in a mesh: seq: 16 (over x_hi, z, core), tp: 8 (over y, x_lo).
Axes of the slice: x: 4 (x_hi: 2, x_lo: 2; x = x_hi * 2 + x_lo), y: 4, z: 4, core: 2. Of those that a mesh axis runs over, the one named last changes fastest.
Arguments:
- tokens: bfloat16 [2048, 8192], P('seq'), may hold values from -6 to 6
- conv_weight: float32 [4, 8192], replicated, may hold values from -3 to 3
- norm_gain: float32 [8192], replicated, may hold values from 0.25 to 1.75
- gate_weight: bfloat16 [8192, 14336], P('seq', 'tp'), may hold values from -0.0625 to 0.0625
- up_weight: bfloat16 [8192, 14336], P('seq', 'tp'), may hold values from -0.0625 to 0.0625
- down_weight: bfloat16 [14336, 8192], P('tp', 'seq'), may hold values from -0.046875 to 0.046875
Outputs:
- mixed_out: bfloat16 [2048, 8192], P(('seq', 'tp'))
All inputs are finite; a program needn't handle non-finite values.
Results may differ from a plain program's by a relative error of at most 0.03.
Values may be sent and summed in bfloat16 or wider, within the bound.
No kernel may reach another device: no remote copies, remote signals or barrier semaphores. Data moves between devices by JAX's collectives and lax.ppermute only.
A program may use at most 64 MiB of HBM per device.

v0:
```python
import jax
import jax.numpy as jnp
from jax import lax
from jax.sharding import PartitionSpec as P


def from_behind(shard, axis, by):
    peers = lax.axis_size(axis)
    pairs = [(i, i + by) for i in range(peers) if 0 <= i + by < peers]
    return lax.ppermute(shard, axis, pairs)


def split_up(shard, dim, peers):
    shape = shard.shape
    parts = shard.reshape(*shape[:dim], peers, shape[dim] // peers, *shape[dim + 1 :])
    return jnp.moveaxis(parts, dim, 0)


def summed_on_arrival(shard, axis, dim):
    parts = split_up(shard, dim, lax.axis_size(axis))
    arrived = lax.all_to_all(parts, axis, split_axis=0, concat_axis=0, tiled=True)
    return arrived.astype(jnp.float32).sum(axis=0)


def swiglu(both_sums, half_cols):
    return (jax.nn.silu(both_sums[:, :half_cols]) * both_sums[:, half_cols:]).astype(jnp.bfloat16)


def shards(tokens, conv_weight, norm_gain, gate_weight, up_weight, down_weight):
    tok_rows = tokens.shape[0]
    taps_count = conv_weight.shape[0]
    seq_count = lax.axis_size("seq")
    edge_rows = from_behind(tokens[tok_rows - (taps_count - 1) :], "seq", 1)
    extended = jnp.concatenate([edge_rows, tokens], 0).astype(jnp.float32)
    conv_out = jnp.zeros(tokens.shape, jnp.float32)
    for tap_index in range(taps_count):
        begin = taps_count - 1 - tap_index
        conv_out = conv_out + conv_weight[tap_index][None, :] * extended[begin : begin + tok_rows]
    scale_rms = lax.rsqrt(jnp.mean(conv_out * conv_out, axis=-1, keepdims=True) + 1e-05)
    normed = (conv_out * scale_rms * norm_gain[None, :]).astype(jnp.bfloat16)
    all_rows = lax.all_to_all(normed, "seq", split_axis=1, concat_axis=0, tiled=True)
    half_cols = gate_weight.shape[1]
    w_both = jnp.concatenate([gate_weight, up_weight], 1)
    gate_share = lax.psum_scatter(
        jnp.dot(all_rows, w_both, preferred_element_type=jnp.float32).astype(jnp.bfloat16),
        "seq",
        scatter_dimension=0,
        tiled=True,
    ).astype(jnp.float32)
    hidden = swiglu(gate_share, half_cols)
    out_terms = jnp.dot(
        lax.all_gather(hidden, "seq", axis=0, tiled=True),
        down_weight,
        preferred_element_type=jnp.float32,
    )
    col_width = out_terms.shape[1]
    out_terms = out_terms.reshape(seq_count, tok_rows, col_width)
    summed = summed_on_arrival(out_terms.astype(jnp.bfloat16), "tp", 1)
    rounded = summed.astype(jnp.bfloat16)
    mixed_out = lax.all_to_all(rounded, "seq", split_axis=0, concat_axis=2, tiled=True)
    return mixed_out.reshape(mixed_out.shape[1], mixed_out.shape[2])


def solution(mesh):
    in_specs = (P("seq", None), P(), P(), P("seq", "tp"), P("seq", "tp"), P("tp", "seq"))
    out_specs = P(("seq", "tp"), None)
    return jax.shard_map(shards, mesh=mesh, in_specs=in_specs, out_specs=out_specs, check_vma=False)
```

profile of v0, /device:TPU:1, one launch (start us, length us, event | category | flops | bytes accessed | tf_op | source)
XLA Modules:
  0.0 350.1 jit_solution(9454202880680602987)
XLA Ops:
  6.5 0.0 copy-start
  6.5 0.0 reduce-scatter.2.cloned.1.call-start
  6.5 1.1 slice.34
  7.6 4.9 %collective-permute-start = (bf16[3,8192]{1,0:T(4,128)(2,1)S(1)}, bf16[3,8192]{1,0:T(4,128)(2,1)S(1)}, u32[]{:S(2)}, u32[]{:S(2)}) collective-permute-start(bf16[3,8192]{1,0:T(4,128)(2,1)S(1)} %slice.34), channel_id=1, source_target_pairs={{0,8},{8,16},{16,24},{24,32},{32,40},{40,48},{48,56},{56,64},{64,7... | collective-permute-start | bytes 147464 | tf_op jit(solution)/shard_map/ppermute | solution.py:10
  12.5 1.4 fusion.9
  13.9 4.1 %copy.16 = bf16[128,8192]{0,1:T(8,128)(2,1)} copy(bf16[128,8192]{1,0:T(8,128)(2,1)} %param.6) | data formatting | bytes 4194304 | tf_op args[0]
  18.0 0.0 collective-permute-done
  18.0 1.8 copy.15
  19.8 3.7 %maximum_convert_fusion = f32[131,8192]{0,1:T(8,128)S(1)} fusion(bf16[128,8192]{0,1:T(8,128)(2,1)} %copy.16, bf16[3,8192]{0,1:T(8,128)(2,1)} %copy.15), kind=kLoop, calls=%fused_computation.8 | loop fusion | flops 4292608 | bytes 6438912 | tf_op jit(solution)/shard_map/convert_element_type | solution.py:34
  23.6 0.0 copy-start.1
  23.6 8.7 %multiply_reduce_fusion = (f32[128]{0:T(128)S(1)}, f32[128,8192]{0,1:T(8,128)S(1)}) fusion(f32[131,8192]{0,1:T(8,128)S(1)} %maximum_convert_fusion, f32[8192]{0:T(1024)S(1)} %bitcast.30, f32[8192]{0:T(1024)S(1)} %bitcast.31, f32[8192]{0:T(1024)S(1)} %bitcast.29, f32[8192]{0:T(1024)S(1)} %bitcast.28), kind=kLoop, calls=%fused_computation.10 | loop fusion | flops 9437056 | bytes 21103104 | tf_op jit(solution)/shard_map/reduce_sum | solution.py:39
  32.3 0.0 copy-done.1
  32.3 3.5 multiply_convert_fusion
  35.8 35.4 %all_to_all.39 = bf16[128,16,512]{0,2,1:T(8,128)(2,1)} all-to-all(bf16[128,16,512]{0,2,1:T(8,128)(2,1)S(1)} %bitcast.22), channel_id=1, replica_groups=mesh['seq'=16,'tp'=8] {'seq'}, dimensions={1} | all-to-all | bytes 4194304 | tf_op jit(solution)/shard_map/all_to_all | solution.py:41
  71.2 3.9 %copy.17 = bf16[16,128,512]{2,1,0:T(8,128)(2,1)} copy(bf16[16,128,512]{1,2,0:T(8,128)(2,1)} %bitcast.23) | data formatting | bytes 4194304 | tf_op jit(solution)/shard_map/all_to_all | solution.py:41
  75.1 13.4 %convolution_convert_fusion = bf16[2048,3584]{1,0:T(8,128)(2,1)} fusion(bf16[2048,512]{1,0:T(8,128)(2,1)} %bitcast.25, bf16[512,1792]{1,0:T(8,128)(2,1)} %param.10, bf16[512,1792]{1,0:T(8,128)(2,1)} %param.9), kind=kOutput, calls=%fused_computation | convolution fusion | flops 7530872832 | bytes 20447232 | tf_op jit(solution)/shard_map/dot_general | solution.py:45
  88.5 0.0 reduce-scatter.2.cloned.1.call-update
  88.5 0.0 all-gather.2.cloned.1.call-start
  88.6 129.9 %reduce-scatter.2.cloned.1.call-done = bf16[128,3584]{1,0:T(8,128)(2,1)} async-done(((bf16[2048,3584]{1,0:T(8,128)(2,1)}), bf16[128,3584]{1,0:T(8,128)(2,1)}) %reduce-scatter.2.cloned.1.call-update) | async-done | bytes 917520 | tf_op jit(solution)/shard_map/reduce_scatter | solution.py:44
  218.4 1.4 convert_element_type.27
  219.8 1.0 fusion.6
  220.8 0.0 all-gather.2.cloned.1.call-update
  220.8 67.8 %all-gather.2.cloned.1.call-done = bf16[2048,1792]{1,0:T(8,128)(2,1)} async-done(((bf16[128,1792]{1,0:T(8,128)(2,1)}), bf16[2048,1792]{1,0:T(8,128)(2,1)}) %all-gather.2.cloned.1.call-update) | async-done | bytes 7340048 | tf_op jit(solution)/shard_map/all_gather | solution.py:52
  288.6 0.0 copy-done
  288.7 7.3 %convolution_convert_fusion.1 = bf16[2048,512]{1,0:T(8,128)(2,1)S(1)} fusion(bf16[2048,1792]{1,0:T(8,128)(2,1)} %all-gather.2.cloned.1.call-done, bf16[1792,512]{1,0:T(8,128)(2,1)S(1)} %copy-done), kind=kOutput, calls=%fused_computation.14 | convolution fusion | flops 3759144960 | bytes 11272192 | tf_op jit(solution)/shard_map/dot_general | solution.py:51
  295.9 0.2 copy.25
  296.1 30.1 %all_to_all.40 = bf16[8,16,16,512]{3,2,1,0:T(8,128)(2,1)} all-to-all(bf16[8,16,16,512]{3,2,1,0:T(8,128)(2,1)S(1)} %bitcast.24), channel_id=1, replica_groups=mesh['seq'=16,'tp'=8] {'tp'}, dimensions={0} | all-to-all | bytes 4194304 | tf_op jit(solution)/shard_map/all_to_all | solution.py:21
  326.2 2.0 reduce_sum.22
  328.2 14.4 %all_to_all.41 = bf16[16,16,512]{2,1,0:T(8,128)(2,1)S(1)} all-to-all(bf16[16,16,512]{2,1,0:T(8,128)(2,1)S(1)} %reduce_sum.22), channel_id=1, replica_groups=mesh['seq'=16,'tp'=8] {'seq'}, dimensions={0} | all-to-all | bytes 524288 | tf_op jit(solution)/shard_map/all_to_all | solution.py:60
  342.6 0.7 copy.22
  (1 shorter events, 0.0 us)
Async XLA Ops:
  6.5 282.1 %copy-start = (bf16[1792,512]{1,0:T(8,128)(2,1)S(1)}, bf16[1792,512]{1,0:T(8,128)(2,1)}, u32[]{:S(2)}) copy-start(bf16[1792,512]{1,0:T(8,128)(2,1)} %param.11) | copy-start | bytes 5505028
  6.5 211.9 %reduce-scatter.2.cloned.1.call-start = ((), (), s32[]{:S(2)}) async-start(), calls=%async_computation.4 | async-start | bytes 15597568 | tf_op jit(solution)/shard_map/reduce_scatter | solution.py:44
  7.6 10.4 %collective-permute-start = (bf16[3,8192]{1,0:T(4,128)(2,1)S(1)}, bf16[3,8192]{1,0:T(4,128)(2,1)S(1)}, u32[]{:S(2)}, u32[]{:S(2)}) collective-permute-start(bf16[3,8192]{1,0:T(4,128)(2,1)S(1)} %slice.34), channel_id=1, source_target_pairs={{0,8},{8,16},{16,24},{24,32},{32,40},{40,48},{48,56},{56,64},{64,7... | collective-permute-start | bytes 147464 | tf_op jit(solution)/shard_map/ppermute | solution.py:10
  23.6 8.8 %copy-start.1 = (f32[8192]{0:T(1024)S(1)}, f32[8192]{0:T(1024)}, u32[]{:S(2)}) copy-start(f32[8192]{0:T(1024)} %param.8) | copy-start | bytes 98308
  88.5 200.1 %all-gather.2.cloned.1.call-start = ((), (), s32[]{:S(2)}) async-start(), calls=%async_computation.5 | async-start | bytes 7798784 | tf_op jit(solution)/shard_map/all_gather | solution.py:52
Sparse Core Ops, SparseCore 0:
  88.6 129.7 reduce-scatter.1
  221.0 67.6 all-gather.1
where the time goes:
time: 351 us; the launch traced here: 350 us
  waiting for transfers between devices  198 us (56%)
  blocking collectives  79.8 us (23%)
  matrix products  20.6 us (6%)
  other arithmetic  20.3 us (6%)
  between operations  13.5 us (4%)
  local copies, waits for them, and re-layouts  13.2 us (4%)
  starting transfers between devices  4.97 us (1%)
    reduce_scatter x1, waiting for transfers between devices, shards(): lax.psum_scatter(jnp.dot(all_rows, w_both, preferred_element_type=jnp.flo...  130 us
    all_gather x1, waiting for transfers between devices, shards(): lax.all_gather(hidden, 'seq', axis=0, tiled=True)  67.8 us
    all_to_all x1, blocking collectives, shards(): lax.all_to_all(normed, 'seq', split_axis=1, concat_axis=0, tiled=True)  35.4 us
    all_to_all x1, blocking collectives, summed_on_arrival(): lax.all_to_all(parts, axis, split_axis=0, concat_axis=0, tiled=True)  30.1 us
    all_to_all x1, blocking collectives, shards(): lax.all_to_all(rounded, 'seq', split_axis=0, concat_axis=2, tiled=True)  14.4 us
    dot_general x1, matrix products, shards(): jnp.dot(all_rows, w_both, preferred_element_type=jnp.float32)  13.4 us
    reduce_sum x1, other arithmetic, shards(): jnp.mean(conv_out * conv_out, axis=-1, keepdims=True) + 1e-05  8.75 us
    dot_general x1, matrix products, shards(): jnp.dot(lax.all_gather(hidden, 'seq', axis=0, tiled=True), down_weight, p...  7.26 us
  transfers between devices with their start and end apart: 3, of which 2 were waited for; matrix products, arithmetic and copies ran while one was open for 2% of the time, Pallas kernels for 0%

commit v1 on v0

--- a/solution.py
+++ b/solution.py
@@ -38,7 +38,10 @@
         conv_out = conv_out + conv_weight[tap_index][None, :] * extended[begin : begin + tok_rows]
     scale_rms = lax.rsqrt(jnp.mean(conv_out * conv_out, axis=-1, keepdims=True) + 1e-05)
     normed = (conv_out * scale_rms * norm_gain[None, :]).astype(jnp.bfloat16)
-    all_rows = lax.all_to_all(normed, "seq", split_axis=1, concat_axis=0, tiled=True)
+    all_rows = jnp.concatenate(
+        lax.all_to_all(jnp.stack(jnp.split(normed, lax.axis_size("seq"), axis=1)), "seq", 0, 0),
+        axis=0,
+    )
     half_cols = gate_weight.shape[1]
     w_both = jnp.concatenate([gate_weight, up_weight], 1)
     gate_share = lax.psum_scatter(

time: 351 us -> 329 us (0.937)
  other arithmetic: 20.3 us -> 9.25 us
  local copies, waits for them, and re-layouts: 13.2 us -> 3.46 us
    reduce_sum x1, other arithmetic: 8.75 us -> 2.21 us  [shards(): jnp.mean(conv_out * conv_out, axis=-1, keepdims=True) + 1e-05]
    all_to_all x1 -> x0, local copies, waits for them, and re-layouts: 3.93 us -> none  [shards(): lax.all_to_all(normed, 'seq', split_axis=1, concat_axis=0, tiled=True)]
    unnamed x6 -> x24, local copies, waits for them, and re-layouts: 4.82 us -> 0.91 us
  transfers between devices with their start and end apart: 3 -> 3, of which waited for: 2 -> 2; matrix products, arithmetic and copies ran while one was open for 2% -> 0% of each run, Pallas kernels for 0% -> 0%
where the time goes in v1:
time: 329 us
  waiting for transfers between devices  198 us (60%)
  blocking collectives  81.3 us (25%)
  matrix products  18.6 us (6%)
  between operations  13.6 us (4%)
  other arithmetic  9.25 us (3%)
  starting transfers between devices  4.97 us (2%)
  local copies, waits for them, and re-layouts  3.46 us (1%)
    reduce_scatter x1, waiting for transfers between devices, shards(): lax.psum_scatter(jnp.dot(all_rows, w_both, preferred_element_type=jnp.flo...  130 us
    all_gather x1, waiting for transfers between devices, shards(): lax.all_gather(hidden, 'seq', axis=0, tiled=True)  67.8 us
    all_to_all x1, blocking collectives, shards(): lax.all_to_all(jnp.stack(jnp.split(normed, lax.axis_size('seq'), axis=1))...  36.8 us
    all_to_all x1, blocking collectives, summed_on_arrival(): lax.all_to_all(parts, axis, split_axis=0, concat_axis=0, tiled=True)  30.1 us
    all_to_all x1, blocking collectives, shards(): lax.all_to_all(rounded, 'seq', split_axis=0, concat_axis=2, tiled=True)  14.4 us
    dot_general x1, matrix products, shards(): jnp.dot(all_rows, w_both, preferred_element_type=jnp.float32)  11.3 us
    dot_general x1, matrix products, shards(): jnp.dot(lax.all_gather(hidden, 'seq', axis=0, tiled=True), down_weight, p...  7.26 us
  transfers between devices with their start and end apart: 3, of which 2 were waited for; matrix products, arithmetic and copies ran while one was open for 0% of the time, Pallas kernels for 0%

profile of v1, /device:TPU:1, one launch (start us, length us, event | category | flops | bytes accessed | tf_op | source)
XLA Modules:
  0.0 329.0 jit_solution(8701469700639723766)
XLA Ops:
  6.5 0.0 copy-start
  6.5 0.0 reduce-scatter.2.cloned.1.call-start
  6.5 1.1 slice.34
  7.6 4.9 %collective-permute-start = (bf16[3,8192]{1,0:T(4,128)(2,1)S(1)}, bf16[3,8192]{1,0:T(4,128)(2,1)S(1)}, u32[]{:S(2)}, u32[]{:S(2)}) collective-permute-start(bf16[3,8192]{1,0:T(4,128)(2,1)S(1)} %slice.34), channel_id=1, source_target_pairs={{0,8},{8,16},{16,24},{24,32},{32,40},{40,48},{48,56},{56,64},{64,7... | collective-permute-start | bytes 147464 | tf_op jit(solution)/shard_map/ppermute | solution.py:10
  12.5 1.3 fusion.25
  13.8 0.0 collective-permute-done
  13.9 2.2 maximum_convert_fusion
  16.1 0.0 copy-start.1
  16.1 2.2 multiply_reduce_fusion
  18.3 0.0 copy-done.1
  18.3 0.5 multiply_convert_fusion
  19.1 0.0 copy-start.2
  19.1 0.0 copy-start.3
  19.1 36.8 %all_to_all.25 = bf16[16,128,512]{2,1,0:T(8,128)(2,1)S(1)} all-to-all(bf16[16,128,512]{2,1,0:T(8,128)(2,1)S(1)} %fusion.7), channel_id=1, replica_groups=mesh['seq'=16,'tp'=8] {'seq'}, dimensions={0} | all-to-all | bytes 4194304 | tf_op jit(solution)/shard_map/all_to_all | solution.py:42
  56.0 0.0 copy-done.2
  56.0 0.0 copy-done.3
  56.0 11.3 %convolution_convert_fusion = bf16[2048,3584]{1,0:T(8,128)(2,1)} fusion(bf16[2048,512]{1,0:T(8,128)(2,1)S(1)} %bitcast.85, bf16[512,1792]{1,0:T(8,128)(2,1)S(1)} %copy-done.2, bf16[512,1792]{1,0:T(8,128)(2,1)S(1)} %copy-done.3), kind=kOutput, calls=%fused_computation | convolution fusion | flops 7530872832 | bytes 20447232 | tf_op jit(solution)/shard_map/dot_general | solution.py:48
  67.3 0.0 reduce-scatter.2.cloned.1.call-update
  67.3 0.0 all-gather.2.cloned.1.call-start
  67.4 129.9 %reduce-scatter.2.cloned.1.call-done = bf16[128,3584]{1,0:T(8,128)(2,1)} async-done(((bf16[2048,3584]{1,0:T(8,128)(2,1)}), bf16[128,3584]{1,0:T(8,128)(2,1)}) %reduce-scatter.2.cloned.1.call-update) | async-done | bytes 917520 | tf_op jit(solution)/shard_map/reduce_scatter | solution.py:47
  197.2 1.4 convert_element_type.27
  198.6 1.0 fusion.6
  199.6 0.0 all-gather.2.cloned.1.call-update
  199.7 67.8 %all-gather.2.cloned.1.call-done = bf16[2048,1792]{1,0:T(8,128)(2,1)} async-done(((bf16[128,1792]{1,0:T(8,128)(2,1)}), bf16[2048,1792]{1,0:T(8,128)(2,1)}) %all-gather.2.cloned.1.call-update) | async-done | bytes 7340048 | tf_op jit(solution)/shard_map/all_gather | solution.py:55
  267.5 0.0 copy-done
  267.5 7.3 %convolution_convert_fusion.1 = bf16[2048,512]{1,0:T(8,128)(2,1)S(1)} fusion(bf16[2048,1792]{1,0:T(8,128)(2,1)} %all-gather.2.cloned.1.call-done, bf16[1792,512]{1,0:T(8,128)(2,1)S(1)} %copy-done), kind=kOutput, calls=%fused_computation.13 | convolution fusion | flops 3759144960 | bytes 11272192 | tf_op jit(solution)/shard_map/dot_general | solution.py:54
  274.7 0.2 copy.16
  274.9 30.1 %all_to_all.26 = bf16[8,16,16,512]{3,2,1,0:T(8,128)(2,1)} all-to-all(bf16[8,16,16,512]{3,2,1,0:T(8,128)(2,1)S(1)} %bitcast.84), channel_id=1, replica_groups=mesh['seq'=16,'tp'=8] {'tp'}, dimensions={0} | all-to-all | bytes 4194304 | tf_op jit(solution)/shard_map/all_to_all | solution.py:21
  305.1 2.0 reduce_sum.22
  307.0 14.4 %all_to_all.27 = bf16[16,16,512]{2,1,0:T(8,128)(2,1)S(1)} all-to-all(bf16[16,16,512]{2,1,0:T(8,128)(2,1)S(1)} %reduce_sum.22), channel_id=1, replica_groups=mesh['seq'=16,'tp'=8] {'seq'}, dimensions={0} | all-to-all | bytes 524288 | tf_op jit(solution)/shard_map/all_to_all | solution.py:63
  321.4 0.7 copy.13
  (17 shorter events, 0.2 us)
Async XLA Ops:
  6.5 260.9 %copy-start = (bf16[1792,512]{1,0:T(8,128)(2,1)S(1)}, bf16[1792,512]{1,0:T(8,128)(2,1)}, u32[]{:S(2)}) copy-start(bf16[1792,512]{1,0:T(8,128)(2,1)} %param.11) | copy-start | bytes 5505028
  6.5 190.7 %reduce-scatter.2.cloned.1.call-start = ((), (), s32[]{:S(2)}) async-start(), calls=%async_computation.4 | async-start | bytes 15597568 | tf_op jit(solution)/shard_map/reduce_scatter | solution.py:47
  7.6 6.2 %collective-permute-start = (bf16[3,8192]{1,0:T(4,128)(2,1)S(1)}, bf16[3,8192]{1,0:T(4,128)(2,1)S(1)}, u32[]{:S(2)}, u32[]{:S(2)}) collective-permute-start(bf16[3,8192]{1,0:T(4,128)(2,1)S(1)} %slice.34), channel_id=1, source_target_pairs={{0,8},{8,16},{16,24},{24,32},{32,40},{40,48},{48,56},{56,64},{64,7... | collective-permute-start | bytes 147464 | tf_op jit(solution)/shard_map/ppermute | solution.py:10
  16.1 2.2 copy-start.1
  19.1 36.9 %copy-start.2 = (bf16[512,1792]{1,0:T(8,128)(2,1)S(1)}, bf16[512,1792]{1,0:T(8,128)(2,1)}, u32[]{:S(2)}) copy-start(bf16[512,1792]{1,0:T(8,128)(2,1)} %param.10) | copy-start | bytes 5505028
  19.1 36.9 %copy-start.3 = (bf16[512,1792]{1,0:T(8,128)(2,1)S(1)}, bf16[512,1792]{1,0:T(8,128)(2,1)}, u32[]{:S(2)}) copy-start(bf16[512,1792]{1,0:T(8,128)(2,1)} %param.9) | copy-start | bytes 5505028
  67.3 200.1 %all-gather.2.cloned.1.call-start = ((), (), s32[]{:S(2)}) async-start(), calls=%async_computation.5 | async-start | bytes 7798784 | tf_op jit(solution)/shard_map/all_gather | solution.py:55
Sparse Core Ops, SparseCore 0:
  67.5 129.7 reduce-scatter.1
  199.8 67.6 all-gather.1
